TPU v7x, 32 devices: a whole 2x2x4 slice. The times are simulated.
32 devices in a mesh: dp: 2 (over y), tm: 4 (over z), rows: 4 (over x, core).
Axes of the slice: x: 2, y: 2, z: 4, core: 2. Of those that a mesh axis runs over, the one named last changes fastest.
Arguments:
- clips: bfloat16 [2, 8, 4, 128, 256], P('dp', 'tm', 'rows'), may hold values from -12 to 12
- weight: bfloat16 [3, 3, 3, 256, 256], replicated, may hold values from -0.078125 to 0.078125
- bias: float32 [256], replicated, may hold values from -1 to 1
- head: float32 [256], replicated, may hold values from -4 to 4
Outputs:
- grad_weight: float32 [3, 3, 3, 256, 256], replicated
- grad_bias: float32 [256], replicated
- grad_head: float32 [256], replicated
All inputs are finite; a program needn't handle non-finite values.
Results may differ from a plain program's by a relative error of at most 0.0003.
Values may be sent and summed in bfloat16 or wider, within the bound.
A program may use at most 128 MiB of HBM per device.

v0:
```python
import jax
import jax.numpy as jnp
from jax import lax
from jax.sharding import PartitionSpec as P

penalty_weight = 0.01


def padded_2(value, sides, width):
    for axis, dim in sides:
        count, length = (lax.axis_size(axis), value.shape[dim])
        up = [(i, (i + 1) % count) for i in range(count - 1)]
        down = [(j, i) for i, j in up]
        last = lax.slice_in_dim(value, length - width, length, axis=dim)
        initial = lax.slice_in_dim(value, 0, width, axis=dim)
        before = lax.ppermute(last, axis, up)
        after = lax.ppermute(initial, axis, down)
        value = jnp.concatenate([before, value, after], axis=dim)
    return value


def conv_offsets(padded, weight, transpose):
    nclip, tpad, rpad, wpad, chans = padded.shape
    frames, rowsn, cols = (tpad - 2, rpad - 2, wpad - 2)
    total = jnp.zeros((nclip * frames * rowsn * cols, weight.shape[4]), jnp.float32)
    for a in range(3):
        for b in range(3):
            for d in range(3):
                if transpose:
                    piece = padded[
                        :, 2 - a : 2 - a + frames, 2 - b : 2 - b + rowsn, 2 - d : 2 - d + cols
                    ]
                    total = total + lax.dot_general(
                        piece.reshape(-1, chans),
                        weight[a, b, d],
                        (((1,), (1,)), ((), ())),
                        preferred_element_type=jnp.float32,
                    )
                else:
                    piece = padded[:, a : a + frames, b : b + rowsn, d : d + cols]
                    total = total + jnp.dot(
                        piece.reshape(-1, chans),
                        weight[a, b, d],
                        preferred_element_type=jnp.float32,
                    )
    return total.reshape(nclip, frames, rowsn, cols, -1)


def correlate(padded, right):
    nclip, tpad, rpad, wpad, chans = padded.shape
    frames, rowsn, cols = (tpad - 2, rpad - 2, wpad - 2)
    right_rows = right.reshape(-1, right.shape[-1])
    blocks = []
    for a in range(3):
        for b in range(3):
            for d in range(3):
                piece = padded[:, a : a + frames, b : b + rowsn, d : d + cols].reshape(-1, chans)
                blocks.append(
                    lax.dot_general(
                        piece,
                        right_rows,
                        (((0,), (0,)), ((), ())),
                        preferred_element_type=jnp.float32,
                    )
                )
    return jnp.stack(blocks).reshape(3, 3, 3, chans, right.shape[-1])


def pad_columns(field):
    return jnp.pad(field, ((0, 0), (0, 0), (0, 0), (1, 1), (0, 0)))


def per_device(clips, weight, bias, head):
    clip_pad = pad_columns(padded_2(clips, (("tm", 1), ("rows", 2)), 1))
    pre = conv_offsets(clip_pad, weight, False) + bias
    sig = jax.nn.sigmoid(pre)
    slope = sig * (1.0 + pre * (1.0 - sig))
    curve = sig * (1.0 - sig) * (2.0 + pre * (1.0 - 2.0 * sig))
    score_grad = (head * slope).astype(jnp.bfloat16)
    score_pad = pad_columns(padded_2(score_grad, (("tm", 1), ("rows", 2)), 1))
    input_grad = conv_offsets(score_pad, weight, True).astype(jnp.bfloat16)
    grad_pad = pad_columns(padded_2(input_grad, (("tm", 1), ("rows", 2)), 1))
    back_grad = penalty_weight * conv_offsets(grad_pad, weight, False)
    pre_grad = back_grad * head * curve
    pre_grad_b = pre_grad.astype(jnp.bfloat16)
    local_weight = penalty_weight * correlate(grad_pad, score_grad) + correlate(
        clip_pad, pre_grad_b
    )
    local_bias = jnp.sum(pre_grad, axis=(0, 1, 2, 3))
    local_head = jnp.sum(back_grad * slope, axis=(0, 1, 2, 3))
    grad_weight, grad_bias, grad_head = lax.psum(
        (local_weight, local_bias, local_head), ("dp", "tm", "rows")
    )
    return (grad_weight, grad_bias, grad_head)


def solution(mesh):
    return jax.shard_map(
        per_device,
        mesh=mesh,
        in_specs=(P("dp", "tm", "rows", None, None), P(), P(), P()),
        out_specs=(P(), P(), P()),
        check_vma=False,
    )
```

profile of v0, /device:TPU:0, one launch (start us, length us, event | category | flops | bytes accessed | tf_op | source)
XLA Modules:
  0.0 416.6 jit_solution(1044394529417805028)
XLA Ops:
  8.3 5.0 %collective-permute-start = (bf16[1,1,1,128,256]{3,4,1,2,0:T(8,128)(2,1)S(1)}, bf16[1,1,1,128,256]{3,4,1,2,0:T(8,128)(2,1)S(1)}, u32[]{:S(2)}, u32[]{:S(2)}) collective-permute-start(bf16[1,1,1,128,256]{3,4,1,2,0:T(8,128)(2,1)S(1)} %get-tuple-element.90), channel_id=1, source_target_pairs={{0,4},{4,8},{8,12},{1,5},{5,9},{9,13},{2,6},{6,10},{10,14},{3,7},{... | collective-permute-start | bytes 196616 | tf_op jit(solution)/shard_map/ppermute | solution.py:16
  15.1 4.3 %collective-permute-done.1 = bf16[1,1,1,128,256]{3,4,1,2,0:T(8,128)(2,1)S(1)} collective-permute-done((bf16[1,1,1,128,256]{3,4,1,2,0:T(8,128)(2,1)S(1)}, bf16[1,1,1,128,256]{3,4,1,2,0:T(8,128)(2,1)S(1)}, u32[]{:S(2)}, u32[]{:S(2)}) %collective-permute-start.1) | collective-permute-done | bytes 65568 | tf_op jit(solution)/shard_map/ppermute | solution.py:17
  23.6 2.3 collective-permute-done.3
  29.3 2.0 fusion.385
  67.0 1.8 fusion.188
  97.1 3.5 collective-permute-start.4
  102.5 4.3 %collective-permute-done.5 = bf16[1,1,1,128,256]{4,3,1,2,0:T(8,128)(2,1)S(1)} collective-permute-done((bf16[1,1,1,128,256]{4,3,1,2,0:T(8,128)(2,1)S(1)}, bf16[1,1,1,128,256]{4,3,1,2,0:T(8,128)(2,1)S(1)}, u32[]{:S(2)}, u32[]{:S(2)}) %collective-permute-start.5) | collective-permute-done | bytes 65568 | tf_op jit(solution)/shard_map/ppermute | solution.py:17
  106.8 5.3 %collective-permute-start.6 = (bf16[1,4,1,128,256]{4,3,1,2,0:T(8,128)(2,1)S(1)}, bf16[1,4,1,128,256]{4,3,1,2,0:T(8,128)(2,1)S(1)}, u32[]{:S(2)}, u32[]{:S(2)}) collective-permute-start(bf16[1,4,1,128,256]{4,3,1,2,0:T(8,128)(2,1)S(1)} %pad_maximum_fusion.1), channel_id=1, source_target_pairs={{0,1},{1,2},{2,3},{4,5},{5,6},{6,7},{8,9},{9,10},{10,11},{12,13},{... | collective-permute-start | bytes 786440 | tf_op jit(solution)/shard_map/ppermute | solution.py:16
  113.4 2.8 collective-permute-done.7
  123.3 3.5 collective-permute-start.8
  128.6 4.3 %collective-permute-done.9 = bf16[1,1,1,128,256]{3,4,1,2,0:T(8,128)(2,1)S(1)} collective-permute-done((bf16[1,1,1,128,256]{3,4,1,2,0:T(8,128)(2,1)S(1)}, bf16[1,1,1,128,256]{3,4,1,2,0:T(8,128)(2,1)S(1)}, u32[]{:S(2)}, u32[]{:S(2)}) %collective-permute-start.9) | collective-permute-done | bytes 65568 | tf_op jit(solution)/shard_map/ppermute | solution.py:17
  132.9 5.2 %collective-permute-start.10 = (bf16[1,4,1,128,256]{3,4,1,2,0:T(8,128)(2,1)S(1)}, bf16[1,4,1,128,256]{3,4,1,2,0:T(8,128)(2,1)S(1)}, u32[]{:S(2)}, u32[]{:S(2)}) collective-permute-start(bf16[1,4,1,128,256]{3,4,1,2,0:T(8,128)(2,1)S(1)} %pad_maximum_fusion.2), channel_id=1, source_target_pairs={{0,1},{1,2},{2,3},{4,5},{5,6},{6,7},{8,9},{9,10},{10,11},{12,13},{... | collective-permute-start | bytes 786440 | tf_op jit(solution)/shard_map/ppermute | solution.py:16
  144.0 2.0 fusion.384
  151.6 3.0 copy-done.5
  154.6 1.8 copy.55
  156.4 1.9 fusion.247
  163.4 1.8 fusion.242
  171.9 1.9 fusion.217
  173.7 1.8 fusion.387
  180.5 1.8 fusion.205
  231.6 4.1 multiply_add_fusion
  235.6 43.6 %all-reduce.3 = (f32[256]{0:T(256)}, f32[256]{0:T(256)}) all-reduce(f32[256]{0:T(256)S(1)} %get-tuple-element.5, f32[256]{0:T(256)S(1)} %get-tuple-element.61), channel_id=1, replica_groups=mesh['dp'=2,'tm'=4,'rows'=4] {'dp','tm','rows'}, use_global_device_ids=true, to_apply=%region_2.3 | all-reduce | flops 512 | bytes 4096 | tf_op jit(solution)/shard_map/psum | solution.py:91
  279.2 123.8 %all-reduce.6.cloned.1.call-done = f32[3,3,3,256,256]{4,3,2,1,0:T(8,128)} async-done(((f32[3,3,3,256,256]{4,3,2,1,0:T(8,128)}), f32[3,3,3,256,256]{4,3,2,1,0:T(8,128)}) %all-reduce.6.cloned.1.call-update) | async-done | bytes 7077904 | tf_op jit(solution)/shard_map/psum | solution.py:91
  403.1 6.7 %copy.139 = f32[3,3,3,256,256]{4,3,2,1,0:T(8,128)} copy(f32[3,3,3,256,256]{4,3,2,1,0:T(8,128)} %all-reduce.6.cloned.1.call-done) | data formatting | bytes 14155776
  (335 shorter events, 162.4 us)
Async XLA Ops:
  7.2 395.9 %all-reduce.6.cloned.1.call-start = ((), (), s32[]{:S(2)}) async-start(), calls=%async_computation | async-start | bytes 14155776 | tf_op jit(solution)/shard_map/psum | solution.py:91
  8.3 6.9 %collective-permute-start = (bf16[1,1,1,128,256]{3,4,1,2,0:T(8,128)(2,1)S(1)}, bf16[1,1,1,128,256]{3,4,1,2,0:T(8,128)(2,1)S(1)}, u32[]{:S(2)}, u32[]{:S(2)}) collective-permute-start(bf16[1,1,1,128,256]{3,4,1,2,0:T(8,128)(2,1)S(1)} %get-tuple-element.90), channel_id=1, source_target_pairs={{0,4},{4,8},{8,12},{1,5},{5,9},{9,13},{2,6},{6,10},{10,14},{3,7},{... | collective-permute-start | bytes 196616 | tf_op jit(solution)/shard_map/ppermute | solution.py:16
  13.2 6.2 %collective-permute-start.1 = (bf16[1,1,1,128,256]{3,4,1,2,0:T(8,128)(2,1)S(1)}, bf16[1,1,1,128,256]{3,4,1,2,0:T(8,128)(2,1)S(1)}, u32[]{:S(2)}, u32[]{:S(2)}) collective-permute-start(bf16[1,1,1,128,256]{3,4,1,2,0:T(8,128)(2,1)S(1)} %get-tuple-element.91), channel_id=1, source_target_pairs={{4,0},{8,4},{12,8},{5,1},{9,5},{13,9},{6,2},{10,6},{14,10},{7,3},{... | collective-permute-start | bytes 196616 | tf_op jit(solution)/shard_map/ppermute | solution.py:17
  19.4 4.2 %collective-permute-start.2 = (bf16[1,4,1,128,256]{3,4,1,2,0:T(8,128)(2,1)S(1)}, bf16[1,4,1,128,256]{3,4,1,2,0:T(8,128)(2,1)S(1)}, u32[]{:S(2)}, u32[]{:S(2)}) collective-permute-start(bf16[1,4,1,128,256]{3,4,1,2,0:T(8,128)(2,1)S(1)} %pad_maximum_fusion), channel_id=1, source_target_pairs={{0,1},{1,2},{2,3},{4,5},{5,6},{6,7},{8,9},{9,10},{10,11},{12,13},{... | collective-permute-start | bytes 786440 | tf_op jit(solution)/shard_map/ppermute | solution.py:16
  20.7 5.1 %collective-permute-start.3 = (bf16[1,4,1,128,256]{3,4,1,2,0:T(8,128)(2,1)S(1)}, bf16[1,4,1,128,256]{3,4,1,2,0:T(8,128)(2,1)S(1)}, u32[]{:S(2)}, u32[]{:S(2)}) collective-permute-start(bf16[1,4,1,128,256]{3,4,1,2,0:T(8,128)(2,1)S(1)} %pad_maximum_fusion), channel_id=1, source_target_pairs={{1,0},{2,1},{3,2},{5,4},{6,5},{7,6},{9,8},{10,9},{11,10},{13,12},{... | collective-permute-start | bytes 786440 | tf_op jit(solution)/shard_map/ppermute | solution.py:17
  29.3 8.8 %copy-start = (bf16[3,3,3,256,256]{4,3,2,1,0:T(8,128)(2,1)S(1)}, bf16[3,3,3,256,256]{4,3,2,1,0:T(8,128)(2,1)}, u32[]{:S(2)}) copy-start(bf16[3,3,3,256,256]{4,3,2,1,0:T(8,128)(2,1)} %param.5) | copy-start | bytes 10616836
  87.3 6.4 %copy-start.23 = (f32[256,256]{1,0:T(8,128)S(1)}, f32[256,256]{1,0:T(8,128)}, u32[]{:S(2)}) copy-start(f32[256,256]{1,0:T(8,128)} %fusion.209) | copy-start | bytes 786436
  87.3 6.5 %copy-start.45 = (bf16[1,2,1,128,256]{4,3,1,2,0:T(8,128)(2,1)S(1)}, bf16[1,2,1,128,256]{4,3,1,2,0:T(8,128)(2,1)}, u32[]{:S(2)}) copy-start(bf16[1,2,1,128,256]{4,3,1,2,0:T(8,128)(2,1)} %copy.33) | copy-start | bytes 393220
  87.3 6.7 %copy-start.36 = (bf16[1,2,1,128,256]{4,3,1,2,0:T(8,128)(2,1)S(1)}, bf16[1,2,1,128,256]{4,3,1,2,0:T(8,128)(2,1)}, u32[]{:S(2)}) copy-start(bf16[1,2,1,128,256]{4,3,1,2,0:T(8,128)(2,1)} %copy.35) | copy-start | bytes 393220
  97.1 5.4 %collective-permute-start.4 = (bf16[1,1,1,128,256]{4,3,1,2,0:T(8,128)(2,1)S(1)}, bf16[1,1,1,128,256]{4,3,1,2,0:T(8,128)(2,1)S(1)}, u32[]{:S(2)}, u32[]{:S(2)}) collective-permute-start(bf16[1,1,1,128,256]{4,3,1,2,0:T(8,128)(2,1)S(1)} %get-tuple-element.86), channel_id=1, source_target_pairs={{0,4},{4,8},{8,12},{1,5},{5,9},{9,13},{2,6},{6,10},{10,14},{3,7},{... | collective-permute-start | bytes 196616 | tf_op jit(solution)/shard_map/ppermute | solution.py:16
  100.6 6.2 %collective-permute-start.5 = (bf16[1,1,1,128,256]{4,3,1,2,0:T(8,128)(2,1)S(1)}, bf16[1,1,1,128,256]{4,3,1,2,0:T(8,128)(2,1)S(1)}, u32[]{:S(2)}, u32[]{:S(2)}) collective-permute-start(bf16[1,1,1,128,256]{4,3,1,2,0:T(8,128)(2,1)S(1)} %get-tuple-element.87), channel_id=1, source_target_pairs={{4,0},{8,4},{12,8},{5,1},{9,5},{13,9},{6,2},{10,6},{14,10},{7,3},{... | collective-permute-start | bytes 196616 | tf_op jit(solution)/shard_map/ppermute | solution.py:17
  106.8 6.6 %collective-permute-start.6 = (bf16[1,4,1,128,256]{4,3,1,2,0:T(8,128)(2,1)S(1)}, bf16[1,4,1,128,256]{4,3,1,2,0:T(8,128)(2,1)S(1)}, u32[]{:S(2)}, u32[]{:S(2)}) collective-permute-start(bf16[1,4,1,128,256]{4,3,1,2,0:T(8,128)(2,1)S(1)} %pad_maximum_fusion.1), channel_id=1, source_target_pairs={{0,1},{1,2},{2,3},{4,5},{5,6},{6,7},{8,9},{9,10},{10,11},{12,13},{... | collective-permute-start | bytes 786440 | tf_op jit(solution)/shard_map/ppermute | solution.py:16
  112.1 4.2 %collective-permute-start.7 = (bf16[1,4,1,128,256]{4,3,1,2,0:T(8,128)(2,1)S(1)}, bf16[1,4,1,128,256]{4,3,1,2,0:T(8,128)(2,1)S(1)}, u32[]{:S(2)}, u32[]{:S(2)}) collective-permute-start(bf16[1,4,1,128,256]{4,3,1,2,0:T(8,128)(2,1)S(1)} %pad_maximum_fusion.1), channel_id=1, source_target_pairs={{1,0},{2,1},{3,2},{5,4},{6,5},{7,6},{9,8},{10,9},{11,10},{13,12},{... | collective-permute-start | bytes 786440 | tf_op jit(solution)/shard_map/ppermute | solution.py:17
  123.1 25.6 %copy-start.12 = (bf16[256,256]{1,0:T(8,128)(2,1)}, bf16[256,256]{1,0:T(8,128)(2,1)S(1)}, u32[]{:S(2)}) copy-start(bf16[256,256]{1,0:T(8,128)(2,1)S(1)} %fusion.87) | copy-start | bytes 393220
  123.3 5.4 %collective-permute-start.8 = (bf16[1,1,1,128,256]{3,4,1,2,0:T(8,128)(2,1)S(1)}, bf16[1,1,1,128,256]{3,4,1,2,0:T(8,128)(2,1)S(1)}, u32[]{:S(2)}, u32[]{:S(2)}) collective-permute-start(bf16[1,1,1,128,256]{3,4,1,2,0:T(8,128)(2,1)S(1)} %get-tuple-element.82), channel_id=1, source_target_pairs={{0,4},{4,8},{8,12},{1,5},{5,9},{9,13},{2,6},{6,10},{10,14},{3,7},{... | collective-permute-start | bytes 196616 | tf_op jit(solution)/shard_map/ppermute | solution.py:16
  126.7 6.2 %collective-permute-start.9 = (bf16[1,1,1,128,256]{3,4,1,2,0:T(8,128)(2,1)S(1)}, bf16[1,1,1,128,256]{3,4,1,2,0:T(8,128)(2,1)S(1)}, u32[]{:S(2)}, u32[]{:S(2)}) collective-permute-start(bf16[1,1,1,128,256]{3,4,1,2,0:T(8,128)(2,1)S(1)} %get-tuple-element.83), channel_id=1, source_target_pairs={{4,0},{8,4},{12,8},{5,1},{9,5},{13,9},{6,2},{10,6},{14,10},{7,3},{... | collective-permute-start | bytes 196616 | tf_op jit(solution)/shard_map/ppermute | solution.py:17
  132.9 8.3 %collective-permute-start.10 = (bf16[1,4,1,128,256]{3,4,1,2,0:T(8,128)(2,1)S(1)}, bf16[1,4,1,128,256]{3,4,1,2,0:T(8,128)(2,1)S(1)}, u32[]{:S(2)}, u32[]{:S(2)}) collective-permute-start(bf16[1,4,1,128,256]{3,4,1,2,0:T(8,128)(2,1)S(1)} %pad_maximum_fusion.2), channel_id=1, source_target_pairs={{0,1},{1,2},{2,3},{4,5},{5,6},{6,7},{8,9},{9,10},{10,11},{12,13},{... | collective-permute-start | bytes 786440 | tf_op jit(solution)/shard_map/ppermute | solution.py:16
  138.2 4.2 %collective-permute-start.11 = (bf16[1,4,1,128,256]{3,4,1,2,0:T(8,128)(2,1)S(1)}, bf16[1,4,1,128,256]{3,4,1,2,0:T(8,128)(2,1)S(1)}, u32[]{:S(2)}, u32[]{:S(2)}) collective-permute-start(bf16[1,4,1,128,256]{3,4,1,2,0:T(8,128)(2,1)S(1)} %pad_maximum_fusion.2), channel_id=1, source_target_pairs={{1,0},{2,1},{3,2},{5,4},{6,5},{7,6},{9,8},{10,9},{11,10},{13,12},{... | collective-permute-start | bytes 786440 | tf_op jit(solution)/shard_map/ppermute | solution.py:17
  141.3 8.7 %copy-start.11 = (bf16[1,4,1,128,256]{3,4,1,2,0:T(8,128)(2,1)}, bf16[1,4,1,128,256]{3,4,1,2,0:T(8,128)(2,1)S(1)}, u32[]{:S(2)}) copy-start(bf16[1,4,1,128,256]{3,4,1,2,0:T(8,128)(2,1)S(1)} %collective-permute-done.10) | copy-start | bytes 786436
  142.4 8.8 %copy-start.10 = (bf16[1,4,1,128,256]{3,4,1,2,0:T(8,128)(2,1)}, bf16[1,4,1,128,256]{3,4,1,2,0:T(8,128)(2,1)S(1)}, u32[]{:S(2)}) copy-start(bf16[1,4,1,128,256]{3,4,1,2,0:T(8,128)(2,1)S(1)} %collective-permute-done.11) | copy-start | bytes 786436
  154.6 31.1 %copy-start.2 = (bf16[3,3,3,256,256]{4,3,2,1,0:T(8,128)(2,1)S(1)}, bf16[3,3,3,256,256]{4,3,2,1,0:T(8,128)(2,1)}, u32[]{:S(2)}) copy-start(bf16[3,3,3,256,256]{4,3,2,1,0:T(8,128)(2,1)} %param.5) | copy-start | bytes 10616836
  185.7 6.5 %copy-start.41 = (bf16[1,2,1,128,256]{4,3,1,2,0:T(8,128)(2,1)S(1)}, bf16[1,2,1,128,256]{4,3,1,2,0:T(8,128)(2,1)}, u32[]{:S(2)}) copy-start(bf16[1,2,1,128,256]{4,3,1,2,0:T(8,128)(2,1)} %copy.67) | copy-start | bytes 393220
  218.6 6.5 %copy-start.38 = (bf16[1,2,1,128,256]{4,3,1,2,0:T(8,128)(2,1)S(1)}, bf16[1,2,1,128,256]{4,3,1,2,0:T(8,128)(2,1)}, u32[]{:S(2)}) copy-start(bf16[1,2,1,128,256]{4,3,1,2,0:T(8,128)(2,1)} %copy.77) | copy-start | bytes 393220
  218.6 6.7 %copy-start.37 = (bf16[1,2,1,128,256]{4,3,1,2,0:T(8,128)(2,1)S(1)}, bf16[1,2,1,128,256]{4,3,1,2,0:T(8,128)(2,1)}, u32[]{:S(2)}) copy-start(bf16[1,2,1,128,256]{4,3,1,2,0:T(8,128)(2,1)} %copy.78) | copy-start | bytes 393220
  (47 other events, 173.9 us)
Sparse Core Ops, SparseCore 0:
  235.8 167.2 all-reduce.5
where the time goes:
time: 419 us; the launch traced here: 417 us
  waiting for transfers between devices  145 us (35%)
  local copies, waits for them, and re-layouts  108 us (26%)
  matrix products  65.3 us (16%)
  blocking collectives  43.6 us (10%)
  starting transfers between devices  31.7 us (8%)
  between operations  15.9 us (4%)
  other arithmetic  7.71 us (2%)
    psum x1, waiting for transfers between devices, per_device(): lax.psum((local_weight, local_bias, local_head), ('dp', 'tm', 'rows'))  124 us
    dot_general x54, matrix products, conv_offsets(): jnp.dot(piece.reshape(-1, chans), weight[a, b, d], preferred_element_type...  48.5 us
    slice x29, local copies, waits for them, and re-layouts, correlate(): piece = padded[:, a:a + frames, b:b + rowsn, d:d + cols].reshape(-1, chans)  47.1 us
    slice x29, local copies, waits for them, and re-layouts, conv_offsets(): piece = padded[:, a:a + frames, b:b + rowsn, d:d + cols]  46.9 us
    psum x1, blocking collectives, per_device(): lax.psum((local_weight, local_bias, local_head), ('dp', 'tm', 'rows'))  43.6 us
    ppermute x6, starting transfers between devices, padded_2(): before = lax.ppermute(last, axis, up)  23.7 us
    ppermute x6, waiting for transfers between devices, padded_2(): after = lax.ppermute(initial, axis, down)  19.1 us
    unnamed x118, local copies, waits for them, and re-layouts  13.2 us
  transfers between devices with their start and end apart: 13, of which 10 were waited for; matrix products, arithmetic and copies ran while one was open for 1% of the time, Pallas kernels for 0%

commit v1 on v0

v1 whole, which is shorter than its diff:
```python
import functools

import jax
import jax.numpy as jnp
from jax import lax
from jax.experimental import pallas as pl
from jax.experimental.pallas import tpu as pltpu
from jax.sharding import PartitionSpec as P

penalty_weight = 0.01
MESH = pl.DeviceIdType.MESH
SUB = 8
TAPS = 3


def factor_groups(sizes):
    dp, tm, rows = sizes
    if rows % 2 == 0:
        pair, far = ("rows", 1, 2), ("rows", 2, rows // 2)
    else:
        pair, far = ("rows", 1, 1), ("rows", 1, rows)
    return pair, far, ("dp", 1, dp), ("tm", 1, tm)


def make_plan(sizes, blocks):
    pair, far, depth, line = factor_groups(sizes)
    orders = [(far, depth, line), (depth, far, line)]
    unit = far[2] * depth[2] * line[2]
    half = -(-blocks // pair[2])
    units = -(-half // unit)
    parts = [(units + k) // len(orders) * unit for k in range(len(orders))]
    return pair, orders, parts, sum(parts) * pair[2]


def kernel(
    sizes, plan, clips_ref, weight_ref, bias_ref, head_ref,
    out_ref, small_ref,
    w_ref, clip_pad, score_pad, grad_pad, acc, slope_ref, curve_ref, cat_s, cat_p, total,
    full, land, small_mine, small_land,
    local_sem, halo_send, halo_recv, part_send, part_recv, gath_send, gath_recv,
    small_send, small_recv,
):
    dp, tm, rows = sizes
    frames, cols, chans = clips_ref.shape
    count = frames * cols
    me = {"dp": lax.axis_index("dp"), "tm": lax.axis_index("tm"), "rows": lax.axis_index("rows")}

    def device(**moved):
        place = dict(me, **moved)
        return (place["dp"], place["tm"], place["rows"])

    weight_copy = pltpu.make_async_copy(weight_ref, w_ref, local_sem.at[0])
    weight_copy.start()
    clip_copy = pltpu.make_async_copy(
        clips_ref, clip_pad.at[pl.ds(1, frames), 1], local_sem.at[1]
    )
    clip_copy.start()
    for pad in (clip_pad, score_pad, grad_pad):
        pad[:, 0] = jnp.zeros((frames + 2, cols, chans), pad.dtype)
        pad[:, 2] = jnp.zeros((frames + 2, cols, chans), pad.dtype)
        pad[0, 1] = jnp.zeros((cols, chans), pad.dtype)
        pad[frames + 1, 1] = jnp.zeros((cols, chans), pad.dtype)

    barrier = pltpu.get_barrier_semaphore()
    flat = me["tm"] * rows + me["rows"]
    plane = tm * rows

    def greet(step, carry):
        other = lax.rem(flat + step, plane)
        pl.semaphore_signal(
            barrier, inc=1, device_id=device(tm=other // rows, rows=lax.rem(other, rows)),
            device_id_type=MESH,
        )
        return carry

    lax.fori_loop(1, plane, greet, 0)
    for step in range(1, dp):
        pl.semaphore_signal(
            barrier, inc=1, device_id=device(dp=lax.rem(me["dp"] + step, dp)), device_id_type=MESH
        )
    pl.semaphore_wait(barrier, plane - 1 + dp - 1)

    moves = [(t, r) for t in (-1, 0, 1) for r in (-1, 0, 1) if (t, r) != (0, 0)]

    def inside(t, r):
        ok = None
        for axis, step, size in (("tm", t, tm), ("rows", r, rows)):
            if step:
                cond = me[axis] > 0 if step < 0 else me[axis] < size - 1
                ok = cond if ok is None else jnp.logical_and(ok, cond)
        return ok

    def halo_copy(which, pad, source, t, r):
        slot = which * len(moves) + moves.index((t, r))
        if t == 0:
            here, there = pl.ds(0, frames), pl.ds(1, frames)
        elif t > 0:
            here, there = pl.ds(frames - 1, 1), pl.ds(0, 1)
        else:
            here, there = pl.ds(0, 1), pl.ds(frames + 1, 1)
        return pltpu.make_async_remote_copy(
            src_ref=source.at[here], dst_ref=pad.at[there, 1 - r],
            send_sem=halo_send.at[slot], recv_sem=halo_recv.at[slot],
            device_id=device(tm=me["tm"] + t, rows=me["rows"] + r), device_id_type=MESH,
        )

    def halo_start(which, pad, source):
        for t, r in moves:
            @pl.when(inside(t, r))
            def _():
                halo_copy(which, pad, source, t, r).start()

    def halo_wait(which, pad, source):
        for t, r in moves:
            @pl.when(inside(t, r))
            def _():
                halo_copy(which, pad, source, t, r).wait_send()

            @pl.when(inside(-t, -r))
            def _():
                halo_copy(which, pad, source, t, r).wait_recv()

    column = lax.rem(lax.broadcasted_iota(jnp.int32, (count, chans), 0), cols)

    def earlier(value):
        return jnp.where(column == 0, 0.0, pltpu.roll(value, 1, 0))

    def later(value):
        return jnp.where(column == cols - 1, 0.0, pltpu.roll(value, count - 1, 0))

    def conv(pad, transpose):
        def step(a, carry):
            base = (TAPS - 1 - a) if transpose else a
            pieces = [
                pad[pl.ds(base, frames), (TAPS - 1 - b) if transpose else b].reshape(count, chans)
                for b in range(TAPS)
            ]
            left = jnp.concatenate(pieces, axis=1)
            for d in range(TAPS):
                taps = [w_ref[(a * TAPS + b) * TAPS + d] for b in range(TAPS)]
                if transpose:
                    part = lax.dot_general(
                        left, jnp.concatenate(taps, axis=1), (((1,), (1,)), ((), ())),
                        preferred_element_type=jnp.float32,
                    )
                else:
                    part = jnp.dot(
                        left, jnp.concatenate(taps, axis=0), preferred_element_type=jnp.float32
                    )
                acc[d] += part
            return carry

        acc[...] = jnp.zeros_like(acc)
        lax.fori_loop(0, TAPS, step, 0)
        if transpose:
            return later(acc[0]) + acc[1] + earlier(acc[2])
        return earlier(acc[0]) + acc[1] + later(acc[2])

    def shifted(value):
        value = value.astype(jnp.float32)
        return jnp.concatenate(
            [later(value), value, earlier(value)], axis=1
        ).astype(jnp.bfloat16)

    halo_start(0, clip_pad, clips_ref)
    clip_copy.wait()
    weight_copy.wait()
    halo_wait(0, clip_pad, clips_ref)
    pre = conv(clip_pad, False) + bias_ref[...]
    sig = jax.nn.sigmoid(pre)
    slope = sig * (1.0 + pre * (1.0 - sig))
    slope_ref[...] = slope
    curve_ref[...] = sig * (1.0 - sig) * (2.0 + pre * (1.0 - 2.0 * sig))
    score = (head_ref[...] * slope).astype(jnp.bfloat16)
    score_pad[pl.ds(1, frames), 1] = score.reshape(frames, cols, chans)
    score_own = score_pad.at[pl.ds(1, frames), 1]
    cat_s[...] = shifted(score)
    halo_start(1, score_pad, score_own)
    halo_wait(1, score_pad, score_own)

    input_grad = conv(score_pad, True).astype(jnp.bfloat16)
    grad_pad[pl.ds(1, frames), 1] = input_grad.reshape(frames, cols, chans)
    grad_own = grad_pad.at[pl.ds(1, frames), 1]
    halo_start(2, grad_pad, grad_own)
    halo_wait(2, grad_pad, grad_own)

    back = penalty_weight * conv(grad_pad, False)
    pre_grad = back * head_ref[...] * curve_ref[...]
    cat_p[...] = shifted(pre_grad.astype(jnp.bfloat16))
    small_mine[...] = jnp.zeros_like(small_mine)
    small_mine[pl.ds(0, 1)] = jnp.sum(pre_grad, axis=0, keepdims=True)
    small_mine[pl.ds(1, 1)] = jnp.sum(back * slope_ref[...], axis=0, keepdims=True)

    pair, orders, parts, padded = plan
    rows_per_tap = chans // SUB

    def correlate(ab, carry):
        a, b = ab // TAPS, lax.rem(ab, TAPS)
        dims = (((0,), (0,)), ((), ()))
        first = lax.dot_general(
            grad_pad[pl.ds(a, frames), b].reshape(count, chans), cat_s[...], dims,
            preferred_element_type=jnp.float32,
        )
        second = lax.dot_general(
            clip_pad[pl.ds(a, frames), b].reshape(count, chans), cat_p[...], dims,
            preferred_element_type=jnp.float32,
        )
        both = penalty_weight * first + second
        for d in range(TAPS):
            total[pl.ds((ab * TAPS + d) * rows_per_tap, rows_per_tap)] = both[
                :, d * chans : (d + 1) * chans
            ].reshape(rows_per_tap, SUB, chans)
        return carry

    lax.fori_loop(0, TAPS * TAPS, correlate, 0)
    used = TAPS**3 * rows_per_tap
    if padded > used:
        total[pl.ds(used, padded - used)] = jnp.zeros((padded - used, SUB, chans), jnp.float32)

    sems = {"part": 0, "gath": 0, "land": 0}

    def place_in(group):
        axis, stride, size = group
        return lax.rem(me[axis] // stride, size)

    def peer(group, step):
        axis, stride, size = group
        mine = place_in(group)
        other = lax.rem(mine + step, size)
        return other, device(**{axis: me[axis] + (other - mine) * stride})

    def scatter_start(group, base, size):
        share = size // group[2]
        copies = []
        for step in range(1, group[2]):
            other, target = peer(group, step)
            copy = pltpu.make_async_remote_copy(
                src_ref=total.at[pl.ds(base + other * share, share)],
                dst_ref=land.at[pl.ds(sems["land"], share)],
                send_sem=part_send.at[sems["part"]], recv_sem=part_recv.at[sems["part"]],
                device_id=target, device_id_type=MESH,
            )
            copy.start()
            copies.append((copy, sems["land"]))
            sems["land"] += share
            sems["part"] += 1
        return copies, base + place_in(group) * share, share

    def scatter_end(copies, base, share, dest):
        for copy, at in copies:
            copy.wait()
        if not copies and dest is total:
            return
        chunk = min(share, 9)
        while share % chunk:
            chunk -= 1

        def add(step, carry):
            here = pl.ds(base + step * chunk, chunk)
            value = total[here]
            for _, at in copies:
                value = value + land[pl.ds(at + step * chunk, chunk)]
            dest[here] = value
            return carry

        lax.fori_loop(0, share // chunk, add, 0)

    def gather_start(group, base, size):
        copies = []
        for step in range(1, group[2]):
            _, target = peer(group, step)
            block = full.at[pl.ds(base, size)]
            copy = pltpu.make_async_remote_copy(
                src_ref=block, dst_ref=block,
                send_sem=gath_send.at[sems["gath"]], recv_sem=gath_recv.at[sems["gath"]],
                device_id=target, device_id_type=MESH,
            )
            copy.start()
            copies.append(copy)
            sems["gath"] += 1
        return copies

    at = 0
    for number, group in enumerate((pair,) + orders[0]):
        copies = []
        for step in range(1, group[2]):
            _, target = peer(group, step)
            copy = pltpu.make_async_remote_copy(
                src_ref=small_mine.at[pl.ds(number * SUB, SUB)],
                dst_ref=small_land.at[pl.ds(at * SUB, SUB)],
                send_sem=small_send.at[at], recv_sem=small_recv.at[at],
                device_id=target, device_id_type=MESH,
            )
            copy.start()
            copies.append((copy, at))
            at += 1
        if number == 0:
            copies_half, half_base, half_size = scatter_start(pair, 0, padded)
            value = small_mine[pl.ds(0, SUB)]
        for copy, _ in copies:
            copy.wait()
        for _, slot in copies:
            value = value + small_land[pl.ds(slot * SUB, SUB)]
        small_mine[pl.ds((number + 1) * SUB, SUB)] = value
    small_ref[...] = value

    scatter_end(copies_half, half_base, half_size, total)
    state = [(half_base + sum(parts[:index]), size) for index, size in enumerate(parts)]
    trail = [[] for _ in orders]
    depth = len(orders[0])
    for level in range(depth):
        started = []
        for index, order in enumerate(orders):
            base, size = state[index]
            trail[index].append((base, size))
            started.append(scatter_start(order[level], base, size))
        for index in range(len(orders)):
            copies, base, share = started[index]
            scatter_end(copies, base, share, full if level == depth - 1 else total)
            state[index] = (base, share)
    for level in reversed(range(depth)):
        started = [
            gather_start(order[level], *state[index]) for index, order in enumerate(orders)
        ]
        for index in range(len(orders)):
            for copy in started[index]:
                copy.wait()
            state[index] = trail[index][level]
    last = []
    for index in range(len(orders)):
        last.extend(gather_start(pair, *state[index]))
    own = pltpu.make_async_copy(
        full.at[pl.ds(half_base, half_size)], out_ref.at[pl.ds(half_base, half_size)],
        local_sem.at[2],
    )
    own.start()
    for copy in last:
        copy.wait()
    own.wait()
    if pair[2] > 1:
        other_base = (1 - place_in(pair)) * half_size
        rest = pltpu.make_async_copy(
            full.at[pl.ds(other_base, half_size)], out_ref.at[pl.ds(other_base, half_size)],
            local_sem.at[3],
        )
        rest.start()
        rest.wait()


def per_device(sizes, clips, weight, bias, head):
    _, frames, _, cols, chans = clips.shape
    count = frames * cols
    used = TAPS**3 * chans // SUB
    plan = make_plan(sizes, used)
    pair, orders, parts, padded = plan
    land = padded // pair[2] * (pair[2] - 1)
    parts_n, small_n = pair[2] - 1, sum(g[2] - 1 for g in (pair,) + orders[0])
    gath_n = (pair[2] - 1) * len(orders)
    for order, size in zip(orders, parts):
        for group in order:
            land += size // group[2] * (group[2] - 1)
            parts_n += group[2] - 1
            gath_n += group[2] - 1
            size //= group[2]
    pad = pltpu.VMEM((frames + 2, 3, cols, chans), jnp.bfloat16)
    field = pltpu.VMEM((count, chans), jnp.float32)
    dma = pltpu.SemaphoreType.DMA
    vmem = pl.BlockSpec(memory_space=pltpu.VMEM)
    hbm = pl.BlockSpec(memory_space=pl.ANY)
    grad_weight, small = pl.pallas_call(
        functools.partial(kernel, sizes, plan),
        out_shape=(
            jax.ShapeDtypeStruct((padded, SUB, chans), jnp.float32),
            jax.ShapeDtypeStruct((SUB, chans), jnp.float32),
        ),
        in_specs=[hbm, hbm, vmem, vmem],
        out_specs=(hbm, vmem),
        scratch_shapes=[
            pltpu.VMEM((TAPS**3, chans, chans), jnp.bfloat16),
            pad, pad, pad,
            pltpu.VMEM((TAPS, count, chans), jnp.float32),
            field, field,
            pltpu.VMEM((count, TAPS * chans), jnp.bfloat16),
            pltpu.VMEM((count, TAPS * chans), jnp.bfloat16),
            pltpu.VMEM((padded, SUB, chans), jnp.float32),
            pltpu.VMEM((padded, SUB, chans), jnp.float32),
            pltpu.VMEM((land, SUB, chans), jnp.float32),
            pltpu.VMEM((5 * SUB, chans), jnp.float32),
            pltpu.VMEM((max(small_n, 1) * SUB, chans), jnp.float32),
            dma((4,)), dma((24,)), dma((24,)),
            dma((max(parts_n, 1),)), dma((max(parts_n, 1),)),
            dma((max(gath_n, 1),)), dma((max(gath_n, 1),)),
            dma((max(small_n, 1),)), dma((max(small_n, 1),)),
        ],
        compiler_params=pltpu.CompilerParams(
            collective_id=0, has_side_effects=True, vmem_limit_bytes=60 * 1024 * 1024
        ),
    )(
        clips.reshape(frames, cols, chans),
        weight.reshape(TAPS**3, chans, chans),
        bias.reshape(1, chans),
        head.reshape(1, chans),
    )
    if padded != used:
        grad_weight = grad_weight[:used]
    return grad_weight.reshape(TAPS, TAPS, TAPS, chans, chans), small[0], small[1]


def solution(mesh):
    sizes = tuple(mesh.shape[axis] for axis in ("dp", "tm", "rows"))
    return jax.shard_map(
        functools.partial(per_device, sizes),
        mesh=mesh,
        in_specs=(P("dp", "tm", "rows", None, None), P(), P(), P()),
        out_specs=(P(), P(), P()),
        check_vma=False,
    )
```

time: 419 us -> 156 us (0.37)
  Pallas kernels: 0 us -> 145 us
  waiting for transfers between devices: 145 us -> 0 us
  local copies, waits for them, and re-layouts: 108 us -> 8.07 us
  matrix products: 65.3 us -> 0 us
  blocking collectives: 43.6 us -> 0 us
  starting transfers between devices: 31.7 us -> 0 us
  between operations: 15.9 us -> 0.64 us
  other arithmetic: 7.71 us -> 0 us
    pallas_call x0 -> x1, Pallas kernels: none -> 145 us  [per_device(): pl.pallas_call(functools.partial(kernel, sizes, plan), out_shape=(jax.Sha...]
    psum x1 -> x0, waiting for transfers between devices: 124 us -> none  [per_device(): lax.psum((local_weight, local_bias, local_head), ('dp', 'tm', 'rows'))]
    slice x64 -> x1, local copies, waits for them, and re-layouts: 94.5 us -> 1.34 us  [per_device(): small[1]]
    dot_general x135 -> x0, matrix products: 65.3 us -> none  [the longest x54 48.5 us: conv_offsets(): jnp.dot(piece.reshape(-1, chans), weight[a, b, d], preferred_element_type...]
    psum x1 -> x0, blocking collectives: 43.6 us -> none  [per_device(): lax.psum((local_weight, local_bias, local_head), ('dp', 'tm', 'rows'))]
    ppermute x12 -> x0, starting transfers between devices: 31.7 us -> none  [the longest x6 23.7 us: padded_2(): before = lax.ppermute(last, axis, up)]
    ppermute x12 -> x0, waiting for transfers between devices: 20.8 us -> none  [the longest x6 19.1 us: padded_2(): after = lax.ppermute(initial, axis, down)]
    unnamed x118 -> x1, local copies, waits for them, and re-layouts: 13.2 us -> 6.73 us
  transfers between devices with their start and end apart: 13 -> 0, of which waited for: 10 -> 0; matrix products, arithmetic and copies ran while one was open for 1% -> 0% of each run, Pallas kernels for 0% -> 0%
where the time goes in v1:
time: 156 us; the launch traced here: 154 us
  Pallas kernels  145 us (93%)
  local copies, waits for them, and re-layouts  8.07 us (5%)
    pallas_call x1, Pallas kernels, per_device(): pl.pallas_call(functools.partial(kernel, sizes, plan), out_shape=(jax.Sha...  145 us
    unnamed x1, local copies, waits for them, and re-layouts  6.73 us

profile of v1, /device:TPU:0, one launch (start us, length us, event | category | flops | bytes accessed | tf_op | source)
XLA Modules:
  0.0 153.9 jit_solution(18253924034474486390)
XLA Ops:
  0.6 145.2 %shard_map.67 = (f32[864,8,256]{2,1,0:T(8,128)}, f32[8,256]{1,0:T(8,128)}) custom-call(bf16[2,128,256]{2,1,0:T(8,128)(2,1)} %bitcast.9, bf16[27,256,256]{2,1,0:T(8,128)(2,1)} %bitcast.8, f32[1,256]{1,0:T(1,128)} %bitcast.10, f32[1,256]{1,0:T(1,128)} %bitcast.11), custom_call_target="tpu_custom_call" | custom-call | tf_op jit(solution)/shard_map/pallas_call | solution.py:370
  145.8 1.3 fusion
  147.2 6.7 %copy.8 = f32[3,3,3,256,256]{4,3,2,1,0:T(8,128)} copy(f32[3,3,3,256,256]{4,3,2,1,0:T(8,128)} %bitcast.7) | data formatting | bytes 14155776

commit v2 on v1

--- a/solution.py
+++ b/solution.py
@@ -1,4 +1,5 @@
 import functools
+import math
 
 import jax
 import jax.numpy as jnp
@@ -11,33 +12,31 @@
 MESH = pl.DeviceIdType.MESH
 SUB = 8
 TAPS = 3
-
-
-def factor_groups(sizes):
+SPAN = 120.0
+
+
+def make_plan(sizes, shares):
     dp, tm, rows = sizes
-    if rows % 2 == 0:
-        pair, far = ("rows", 1, 2), ("rows", 2, rows // 2)
-    else:
-        pair, far = ("rows", 1, 1), ("rows", 1, rows)
-    return pair, far, ("dp", 1, dp), ("tm", 1, tm)
-
-
-def make_plan(sizes, blocks):
-    pair, far, depth, line = factor_groups(sizes)
-    orders = [(far, depth, line), (depth, far, line)]
-    unit = far[2] * depth[2] * line[2]
-    half = -(-blocks // pair[2])
-    units = -(-half // unit)
-    parts = [(units + k) // len(orders) * unit for k in range(len(orders))]
-    return pair, orders, parts, sum(parts) * pair[2]
+    cuts, rest, left = [], [], shares
+    near = 2 if rows % 2 == 0 else 1
+    for axis, stride, count in (("rows", 1, near), ("rows", near, rows // near), ("dp", 1, dp), ("tm", 1, tm)):
+        cut = 1
+        while count % (2 * cut) == 0 and left % (2 * cut) == 0:
+            cut *= 2
+        left //= cut
+        cuts.append((axis, stride, cut))
+        rest.append((axis, stride * cut, count // cut))
+    pair, far, depth, line = cuts
+    rest = tuple(group for group in rest if group[2] > 1)
+    return pair, ((far, depth, line), (depth, far, line)), rest
 
 
 def kernel(
     sizes, plan, clips_ref, weight_ref, bias_ref, head_ref,
     out_ref, small_ref,
     w_ref, clip_pad, score_pad, grad_pad, acc, slope_ref, curve_ref, cat_s, cat_p, total,
-    full, land, small_mine, small_land,
-    local_sem, halo_send, halo_recv, part_send, part_recv, gath_send, gath_recv,
+    land_pair, code, land, full, small_mine, small_land,
+    local_sem, halo_send, halo_recv, pair_send, pair_recv, part_send, part_recv, gath_send, gath_recv,
     small_send, small_recv,
 ):
     dp, tm, rows = sizes
@@ -191,8 +190,30 @@
     small_mine[pl.ds(0, 1)] = jnp.sum(pre_grad, axis=0, keepdims=True)
     small_mine[pl.ds(1, 1)] = jnp.sum(back * slope_ref[...], axis=0, keepdims=True)
 
-    pair, orders, parts, padded = plan
-    rows_per_tap = chans // SUB
+    pair, orders, rest = plan
+    parts, shares, taps = total.shape[:3]
+    lanes = chans // parts
+    half = shares // pair[2]
+    units = chans // SUB
+
+    def place_in(group):
+        axis, stride, size = group
+        return lax.rem(me[axis] // stride, size)
+
+    def peer(group, step):
+        axis, stride, size = group
+        mine = place_in(group)
+        other = lax.rem(mine + step, size)
+        return other, device(**{axis: me[axis] + (other - mine) * stride})
+
+    def pair_copy(ab):
+        other, target = peer(pair, 1)
+        here = pl.ds(ab * TAPS, TAPS)
+        return pltpu.make_async_remote_copy(
+            src_ref=total.at[:, pl.ds(other * half, half), here], dst_ref=land_pair.at[:, :, here],
+            send_sem=pair_send.at[ab], recv_sem=pair_recv.at[ab],
+            device_id=target, device_id_type=MESH,
+        )
 
     def correlate(ab, carry):
         a, b = ab // TAPS, lax.rem(ab, TAPS)
@@ -207,69 +228,89 @@
         )
         both = penalty_weight * first + second
         for d in range(TAPS):
-            total[pl.ds((ab * TAPS + d) * rows_per_tap, rows_per_tap)] = both[
-                :, d * chans : (d + 1) * chans
-            ].reshape(rows_per_tap, SUB, chans)
+            for p in range(parts):
+                at = d * chans + p * lanes
+                total[p, :, ab * TAPS + d] = both[:, at : at + lanes].reshape(units, SUB, lanes)
+        if pair[2] > 1:
+            @pl.when(ab > 0)
+            def _():
+                pair_copy(ab - 1).start()
         return carry
 
     lax.fori_loop(0, TAPS * TAPS, correlate, 0)
-    used = TAPS**3 * rows_per_tap
-    if padded > used:
-        total[pl.ds(used, padded - used)] = jnp.zeros((padded - used, SUB, chans), jnp.float32)
+
+    def finish_pair():
+        if pair[2] == 1:
+            return
+        pair_copy(TAPS * TAPS - 1).start()
+        mine = place_in(pair) * half
+
+        def wait(ab, carry):
+            pair_copy(ab).wait()
+            return carry
+
+        lax.fori_loop(0, TAPS * TAPS, wait, 0)
+
+        def add(step, carry):
+            for p in range(parts):
+                total[p, mine + step] = total[p, mine + step] + land_pair[p, step]
+            return carry
+
+        lax.fori_loop(0, half, add, 0)
+
+    def encode(value):
+        top = (jnp.max(jnp.abs(value), axis=0) * 1.01 + 1e-30).astype(jnp.bfloat16)
+        rate = SPAN / top.astype(jnp.float32)
+        return jnp.exp2(value * rate[None]).astype(jnp.bfloat16), top
 
     sems = {"part": 0, "gath": 0, "land": 0}
 
-    def place_in(group):
-        axis, stride, size = group
-        return lax.rem(me[axis] // stride, size)
-
-    def peer(group, step):
-        axis, stride, size = group
-        mine = place_in(group)
-        other = lax.rem(mine + step, size)
-        return other, device(**{axis: me[axis] + (other - mine) * stride})
-
-    def scatter_start(group, base, size):
-        share = size // group[2]
+    def scatter_start(p, group, base, size, whole=False):
+        share = size if whole else size // group[2]
         copies = []
         for step in range(1, group[2]):
             other, target = peer(group, step)
+            origin = base if whole else base + other * share
+            at = sems["land"]
+
+            def fill(k, carry):
+                value, top = encode(total[p, origin + k])
+                code[at + k, pl.ds(0, taps)] = value
+                code[at + k, taps] = top
+                return carry
+
+            lax.fori_loop(0, share, fill, 0)
             copy = pltpu.make_async_remote_copy(
-                src_ref=total.at[pl.ds(base + other * share, share)],
-                dst_ref=land.at[pl.ds(sems["land"], share)],
+                src_ref=code.at[pl.ds(at, share)], dst_ref=land.at[pl.ds(at, share)],
                 send_sem=part_send.at[sems["part"]], recv_sem=part_recv.at[sems["part"]],
                 device_id=target, device_id_type=MESH,
             )
             copy.start()
-            copies.append((copy, sems["land"]))
+            copies.append((copy, at))
             sems["land"] += share
             sems["part"] += 1
-        return copies, base + place_in(group) * share, share
-
-    def scatter_end(copies, base, share, dest):
-        for copy, at in copies:
+        return copies, base if whole else base + place_in(group) * share, share
+
+    def scatter_end(p, copies, base, share):
+        for copy, _ in copies:
             copy.wait()
-        if not copies and dest is total:
+        if not copies:
             return
-        chunk = min(share, 9)
-        while share % chunk:
-            chunk -= 1
 
         def add(step, carry):
-            here = pl.ds(base + step * chunk, chunk)
-            value = total[here]
+            value = total[p, base + step]
             for _, at in copies:
-                value = value + land[pl.ds(at + step * chunk, chunk)]
-            dest[here] = value
+                value = value + decode(land[at + step], taps)
+            total[p, base + step] = value
             return carry
 
-        lax.fori_loop(0, share // chunk, add, 0)
-
-    def gather_start(group, base, size):
+        lax.fori_loop(0, share, add, 0)
+
+    def gather_start(p, group, base, size):
         copies = []
         for step in range(1, group[2]):
             _, target = peer(group, step)
-            block = full.at[pl.ds(base, size)]
+            block = full.at[p, pl.ds(base, size)]
             copy = pltpu.make_async_remote_copy(
                 src_ref=block, dst_ref=block,
                 send_sem=gath_send.at[sems["gath"]], recv_sem=gath_recv.at[sems["gath"]],
@@ -280,8 +321,13 @@
             sems["gath"] += 1
         return copies
 
-    at = 0
-    for number, group in enumerate((pair,) + orders[0]):
+    finish_pair()
+    base = place_in(pair) * half
+    state = [(base, half)] * parts
+    trail = [[] for _ in range(parts)]
+    depth = len(orders[0])
+
+    def small_start(number, group, at):
         copies = []
         for step in range(1, group[2]):
             _, target = peer(group, step)
@@ -294,100 +340,130 @@
             copy.start()
             copies.append((copy, at))
             at += 1
-        if number == 0:
-            copies_half, half_base, half_size = scatter_start(pair, 0, padded)
-            value = small_mine[pl.ds(0, SUB)]
+        return copies
+
+    def small_end(number, copies):
+        value = small_mine[pl.ds(number * SUB, SUB)]
         for copy, _ in copies:
             copy.wait()
         for _, slot in copies:
             value = value + small_land[pl.ds(slot * SUB, SUB)]
         small_mine[pl.ds((number + 1) * SUB, SUB)] = value
-    small_ref[...] = value
-
-    scatter_end(copies_half, half_base, half_size, total)
-    state = [(half_base + sum(parts[:index]), size) for index, size in enumerate(parts)]
-    trail = [[] for _ in orders]
-    depth = len(orders[0])
-    for level in range(depth):
+
+    small_groups = (pair,) + orders[0] + rest
+    small_at = 0
+    steps = [[order[level] for order in orders] for level in range(depth)]
+    steps += [[group] * parts for group in rest]
+    for level, groups in enumerate(steps):
+        whole = level >= depth
         started = []
-        for index, order in enumerate(orders):
-            base, size = state[index]
-            trail[index].append((base, size))
-            started.append(scatter_start(order[level], base, size))
-        for index in range(len(orders)):
-            copies, base, share = started[index]
-            scatter_end(copies, base, share, full if level == depth - 1 else total)
-            state[index] = (base, share)
+        for p, group in enumerate(groups):
+            if not whole:
+                trail[p].append(state[p])
+            started.append(scatter_start(p, group, *state[p], whole))
+        small = small_start(level, small_groups[level], small_at)
+        small_at += len(small)
+        for p in range(parts):
+            copies, base, share = started[p]
+            scatter_end(p, copies, base, share)
+            state[p] = (base, share)
+        small_end(level, small)
+    for p in range(parts):
+        base, size = state[p]
+
+        def keep(k, carry):
+            value, top = encode(total[p, base + k])
+            full[p, base + k, pl.ds(0, taps)] = value
+            full[p, base + k, taps] = top
+            return carry
+
+        lax.fori_loop(0, size, keep, 0)
+    last_small = len(steps)
+    small = small_start(last_small, small_groups[last_small], small_at)
     for level in reversed(range(depth)):
-        started = [
-            gather_start(order[level], *state[index]) for index, order in enumerate(orders)
-        ]
-        for index in range(len(orders)):
-            for copy in started[index]:
+        started = [gather_start(p, orders[p][level], *state[p]) for p in range(parts)]
+        for p in range(parts):
+            for copy in started[p]:
                 copy.wait()
-            state[index] = trail[index][level]
+            state[p] = trail[p][level]
+    small_end(last_small, small)
+    small_ref[...] = small_mine[pl.ds((last_small + 1) * SUB, SUB)]
     last = []
-    for index in range(len(orders)):
-        last.extend(gather_start(pair, *state[index]))
-    own = pltpu.make_async_copy(
-        full.at[pl.ds(half_base, half_size)], out_ref.at[pl.ds(half_base, half_size)],
-        local_sem.at[2],
-    )
+    for p in range(parts):
+        last.extend(gather_start(p, pair, *state[p]))
+    here = pl.ds(place_in(pair) * half, half)
+    own = pltpu.make_async_copy(full.at[:, here], out_ref.at[:, here], local_sem.at[2])
     own.start()
     for copy in last:
         copy.wait()
+    if pair[2] > 1:
+        there = pl.ds((1 - place_in(pair)) * half, half)
+        other = pltpu.make_async_copy(full.at[:, there], out_ref.at[:, there], local_sem.at[3])
+        other.start()
+        other.wait()
     own.wait()
-    if pair[2] > 1:
-        other_base = (1 - place_in(pair)) * half_size
-        rest = pltpu.make_async_copy(
-            full.at[pl.ds(other_base, half_size)], out_ref.at[pl.ds(other_base, half_size)],
-            local_sem.at[3],
-        )
-        rest.start()
-        rest.wait()
+
+
+def decode(block, taps):
+    unit = block[taps].astype(jnp.float32) * (1.0 / (SPAN * math.log(2.0)))
+    return jnp.log(block[:taps].astype(jnp.float32)) * unit[None]
+
+
+def decode_kernel(code_ref, out_ref):
+    parts, shares, blocks, _, lanes = code_ref.shape
+    for p in range(parts):
+        for k in range(shares):
+            out_ref[:, k, :, p * lanes : (p + 1) * lanes] = decode(code_ref[p, k], blocks - 1)
 
 
 def per_device(sizes, clips, weight, bias, head):
     _, frames, _, cols, chans = clips.shape
     count = frames * cols
-    used = TAPS**3 * chans // SUB
-    plan = make_plan(sizes, used)
-    pair, orders, parts, padded = plan
-    land = padded // pair[2] * (pair[2] - 1)
-    parts_n, small_n = pair[2] - 1, sum(g[2] - 1 for g in (pair,) + orders[0])
-    gath_n = (pair[2] - 1) * len(orders)
-    for order, size in zip(orders, parts):
+    taps, shares, parts = TAPS**3, chans // SUB, 2
+    lanes = chans // parts
+    plan = make_plan(sizes, shares)
+    pair, orders, rest = plan
+    half = shares // pair[2]
+    small_n = sum(g[2] - 1 for g in (pair,) + orders[0] + rest)
+    land = parts_n = gath_n = 0
+    for order in orders:
+        size = half
         for group in order:
             land += size // group[2] * (group[2] - 1)
+            size //= group[2]
             parts_n += group[2] - 1
-            gath_n += group[2] - 1
-            size //= group[2]
+        for group in rest:
+            land += size * (group[2] - 1)
+            parts_n += group[2] - 1
+        gath_n += sum(g[2] - 1 for g in order) + pair[2] - 1
     pad = pltpu.VMEM((frames + 2, 3, cols, chans), jnp.bfloat16)
     field = pltpu.VMEM((count, chans), jnp.float32)
+    coded = pltpu.VMEM((max(land, 1), taps + 1, SUB, lanes), jnp.bfloat16)
     dma = pltpu.SemaphoreType.DMA
     vmem = pl.BlockSpec(memory_space=pltpu.VMEM)
     hbm = pl.BlockSpec(memory_space=pl.ANY)
-    grad_weight, small = pl.pallas_call(
+    code, small = pl.pallas_call(
         functools.partial(kernel, sizes, plan),
         out_shape=(
-            jax.ShapeDtypeStruct((padded, SUB, chans), jnp.float32),
+            jax.ShapeDtypeStruct((parts, shares, taps + 1, SUB, lanes), jnp.bfloat16),
             jax.ShapeDtypeStruct((SUB, chans), jnp.float32),
         ),
         in_specs=[hbm, hbm, vmem, vmem],
         out_specs=(hbm, vmem),
         scratch_shapes=[
-            pltpu.VMEM((TAPS**3, chans, chans), jnp.bfloat16),
+            pltpu.VMEM((taps, chans, chans), jnp.bfloat16),
             pad, pad, pad,
             pltpu.VMEM((TAPS, count, chans), jnp.float32),
             field, field,
             pltpu.VMEM((count, TAPS * chans), jnp.bfloat16),
             pltpu.VMEM((count, TAPS * chans), jnp.bfloat16),
-            pltpu.VMEM((padded, SUB, chans), jnp.float32),
-            pltpu.VMEM((padded, SUB, chans), jnp.float32),
-            pltpu.VMEM((land, SUB, chans), jnp.float32),
-            pltpu.VMEM((5 * SUB, chans), jnp.float32),
+            pltpu.VMEM((parts, shares, taps, SUB, lanes), jnp.float32),
+            pltpu.VMEM((parts, half, taps, SUB, lanes), jnp.float32),
+            coded, coded,
+            pltpu.VMEM((parts, shares, taps + 1, SUB, lanes), jnp.bfloat16),
+            pltpu.VMEM(((len(rest) + 6) * SUB, chans), jnp.float32),
             pltpu.VMEM((max(small_n, 1) * SUB, chans), jnp.float32),
-            dma((4,)), dma((24,)), dma((24,)),
+            dma((4,)), dma((24,)), dma((24,)), dma((TAPS**2,)), dma((TAPS**2,)),
             dma((max(parts_n, 1),)), dma((max(parts_n, 1),)),
             dma((max(gath_n, 1),)), dma((max(gath_n, 1),)),
             dma((max(small_n, 1),)), dma((max(small_n, 1),)),
@@ -397,12 +473,18 @@
         ),
     )(
         clips.reshape(frames, cols, chans),
-        weight.reshape(TAPS**3, chans, chans),
+        weight.reshape(taps, chans, chans),
         bias.reshape(1, chans),
         head.reshape(1, chans),
     )
-    if padded != used:
-        grad_weight = grad_weight[:used]
+    step = math.gcd(shares, 4)
+    grad_weight = pl.pallas_call(
+        decode_kernel,
+        out_shape=jax.ShapeDtypeStruct((taps, shares, SUB, chans), jnp.float32),
+        grid=(shares // step,),
+        in_specs=[pl.BlockSpec((parts, step, taps + 1, SUB, lanes), lambda i: (0, i, 0, 0, 0))],
+        out_specs=pl.BlockSpec((taps, step, SUB, chans), lambda i: (0, i, 0, 0)),
+    )(code)
     return grad_weight.reshape(TAPS, TAPS, TAPS, chans, chans), small[0], small[1]
 
 

time: 156 us -> 108 us (0.69)
  Pallas kernels: 145 us -> 105 us
  local copies, waits for them, and re-layouts: 8.07 us -> 1.34 us
    pallas_call x1, Pallas kernels: 145 us -> 98 us  [per_device(): pl.pallas_call(functools.partial(kernel, sizes, plan), out_shape=(jax.Sha...]
    pallas_call x0 -> x1, Pallas kernels: none -> 7.17 us  [per_device(): pl.pallas_call(decode_kernel, out_shape=jax.ShapeDtypeStruct((taps, share...]
    unnamed x1 -> x0, local copies, waits for them, and re-layouts: 6.73 us -> none
where the time goes in v2:
time: 108 us; the launch traced here: 107 us
  Pallas kernels  105 us (97%)
  local copies, waits for them, and re-layouts  1.34 us (1%)
    pallas_call x1, Pallas kernels, per_device(): pl.pallas_call(functools.partial(kernel, sizes, plan), out_shape=(jax.Sha...  98 us
    pallas_call x1, Pallas kernels, per_device(): pl.pallas_call(decode_kernel, out_shape=jax.ShapeDtypeStruct((taps, share...  7.17 us

profile of v2, /device:TPU:0, one launch (start us, length us, event | category | flops | bytes accessed | tf_op | source)
XLA Modules:
  0.0 107.1 jit_solution(9307318473602818121)
XLA Ops:
  0.6 98.0 %shard_map.67 = (bf16[2,32,28,8,128]{4,3,2,1,0:T(8,128)(2,1)}, f32[8,256]{1,0:T(8,128)}) custom-call(bf16[2,128,256]{2,1,0:T(8,128)(2,1)} %bitcast.9, bf16[27,256,256]{2,1,0:T(8,128)(2,1)} %bitcast.8, f32[1,256]{1,0:T(1,128)} %bitcast.10, f32[1,256]{1,0:T(1,128)} %bitcast.11), custom_call_target="tpu_custom_call" | custom-call | tf_op jit(solution)/shard_map/pallas_call | solution.py:445
  98.6 1.3 %fusion = (f32[1,256]{1,0:T(1,128)}, f32[1,256]{1,0:T(1,128)}) fusion(f32[8,256]{1,0:T(8,128)} %get-tuple-element.6), kind=kLoop, calls=%fused_computation | loop fusion | bytes 4096 | tf_op jit(solution)/shard_map/slice | solution.py:488
  100.0 7.2 %shard_map.68 = f32[27,32,8,256]{3,2,1,0:T(8,128)} custom-call(bf16[2,32,28,8,128]{4,3,2,1,0:T(8,128)(2,1)} %get-tuple-element.5.code_ref), custom_call_target="tpu_custom_call" | custom-call | tf_op jit(solution)/shard_map/pallas_call | solution.py:481

commit v3 on v2

--- a/solution.py
+++ b/solution.py
@@ -28,17 +28,19 @@
         rest.append((axis, stride * cut, count // cut))
     pair, far, depth, line = cuts
     rest = tuple(group for group in rest if group[2] > 1)
-    return pair, ((far, depth, line), (depth, far, line)), rest
+    across, along, ahead = (far, depth, line), (depth, far, line), (line, depth, far)
+    return pair, (ahead, along, across, along, across, across), rest
 
 
 def kernel(
     sizes, plan, clips_ref, weight_ref, bias_ref, head_ref,
-    out_ref, small_ref,
+    out_ref, bias_out, head_out,
     w_ref, clip_pad, score_pad, grad_pad, acc, slope_ref, curve_ref, cat_s, cat_p, total,
     land_pair, code, land, full, small_mine, small_land,
     local_sem, halo_send, halo_recv, pair_send, pair_recv, part_send, part_recv, gath_send, gath_recv,
-    small_send, small_recv,
+    small_send, small_recv, out_sem,
 ):
+    small_refs = (bias_out, head_out)
     dp, tm, rows = sizes
     frames, cols, chans = clips_ref.shape
     count = frames * cols
@@ -109,8 +111,11 @@
             def _():
                 halo_copy(which, pad, source, t, r).start()
 
-    def halo_wait(which, pad, source):
+    def halo_wait(which, pad, source, level):
         for t, r in moves:
+            if (t == 0) != level:
+                continue
+
             @pl.when(inside(t, r))
             def _():
                 halo_copy(which, pad, source, t, r).wait_send()
@@ -127,8 +132,8 @@
     def later(value):
         return jnp.where(column == cols - 1, 0.0, pltpu.roll(value, count - 1, 0))
 
-    def conv(pad, transpose):
-        def step(a, carry):
+    def conv(which, pad, source, transpose):
+        def step(a):
             base = (TAPS - 1 - a) if transpose else a
             pieces = [
                 pad[pl.ds(base, frames), (TAPS - 1 - b) if transpose else b].reshape(count, chans)
@@ -146,11 +151,13 @@
                     part = jnp.dot(
                         left, jnp.concatenate(taps, axis=0), preferred_element_type=jnp.float32
                     )
-                acc[d] += part
-            return carry
-
-        acc[...] = jnp.zeros_like(acc)
-        lax.fori_loop(0, TAPS, step, 0)
+                acc[d] = part if a == 1 else acc[d] + part
+
+        halo_wait(which, pad, source, True)
+        step(1)
+        halo_wait(which, pad, source, False)
+        step(0)
+        step(2)
         if transpose:
             return later(acc[0]) + acc[1] + earlier(acc[2])
         return earlier(acc[0]) + acc[1] + later(acc[2])
@@ -164,8 +171,7 @@
     halo_start(0, clip_pad, clips_ref)
     clip_copy.wait()
     weight_copy.wait()
-    halo_wait(0, clip_pad, clips_ref)
-    pre = conv(clip_pad, False) + bias_ref[...]
+    pre = conv(0, clip_pad, clips_ref, False) + bias_ref[...]
     sig = jax.nn.sigmoid(pre)
     slope = sig * (1.0 + pre * (1.0 - sig))
     slope_ref[...] = slope
@@ -175,15 +181,13 @@
     score_own = score_pad.at[pl.ds(1, frames), 1]
     cat_s[...] = shifted(score)
     halo_start(1, score_pad, score_own)
-    halo_wait(1, score_pad, score_own)
-
-    input_grad = conv(score_pad, True).astype(jnp.bfloat16)
+
+    input_grad = conv(1, score_pad, score_own, True).astype(jnp.bfloat16)
     grad_pad[pl.ds(1, frames), 1] = input_grad.reshape(frames, cols, chans)
     grad_own = grad_pad.at[pl.ds(1, frames), 1]
     halo_start(2, grad_pad, grad_own)
-    halo_wait(2, grad_pad, grad_own)
-
-    back = penalty_weight * conv(grad_pad, False)
+
+    back = penalty_weight * conv(2, grad_pad, grad_own, False)
     pre_grad = back * head_ref[...] * curve_ref[...]
     cat_p[...] = shifted(pre_grad.astype(jnp.bfloat16))
     small_mine[...] = jnp.zeros_like(small_mine)
@@ -192,7 +196,8 @@
 
     pair, orders, rest = plan
     parts, shares, taps = total.shape[:3]
-    lanes = chans // parts
+    lanes = land.shape[-1]
+    split = chans // lanes
     half = shares // pair[2]
     units = chans // SUB
 
@@ -206,53 +211,47 @@
         other = lax.rem(mine + step, size)
         return other, device(**{axis: me[axis] + (other - mine) * stride})
 
-    def pair_copy(ab):
+    def pair_copy(a):
         other, target = peer(pair, 1)
-        here = pl.ds(ab * TAPS, TAPS)
+        here = pl.ds(a * split, split)
         return pltpu.make_async_remote_copy(
-            src_ref=total.at[:, pl.ds(other * half, half), here], dst_ref=land_pair.at[:, :, here],
-            send_sem=pair_send.at[ab], recv_sem=pair_recv.at[ab],
+            src_ref=total.at[here, pl.ds(other * half, half)], dst_ref=land_pair.at[here],
+            send_sem=pair_send.at[a], recv_sem=pair_recv.at[a],
             device_id=target, device_id_type=MESH,
         )
 
-    def correlate(ab, carry):
-        a, b = ab // TAPS, lax.rem(ab, TAPS)
-        dims = (((0,), (0,)), ((), ()))
-        first = lax.dot_general(
-            grad_pad[pl.ds(a, frames), b].reshape(count, chans), cat_s[...], dims,
-            preferred_element_type=jnp.float32,
-        )
-        second = lax.dot_general(
-            clip_pad[pl.ds(a, frames), b].reshape(count, chans), cat_p[...], dims,
-            preferred_element_type=jnp.float32,
-        )
-        both = penalty_weight * first + second
-        for d in range(TAPS):
-            for p in range(parts):
-                at = d * chans + p * lanes
-                total[p, :, ab * TAPS + d] = both[:, at : at + lanes].reshape(units, SUB, lanes)
+    def correlate(a):
+        def step(b, carry):
+            dims = (((0,), (0,)), ((), ()))
+            first = lax.dot_general(
+                grad_pad[a : a + frames, b].reshape(count, chans), cat_s[...], dims,
+                preferred_element_type=jnp.float32,
+            )
+            second = lax.dot_general(
+                clip_pad[a : a + frames, b].reshape(count, chans), cat_p[...], dims,
+                preferred_element_type=jnp.float32,
+            )
+            both = penalty_weight * first + second
+            for d in range(TAPS):
+                for p in range(split):
+                    at = d * chans + p * lanes
+                    total[a * split + p, :, b * TAPS + d] = both[:, at : at + lanes].reshape(
+                        units, SUB, lanes
+                    )
+            return carry
+
+        lax.fori_loop(0, TAPS, step, 0)
         if pair[2] > 1:
-            @pl.when(ab > 0)
-            def _():
-                pair_copy(ab - 1).start()
-        return carry
-
-    lax.fori_loop(0, TAPS * TAPS, correlate, 0)
-
-    def finish_pair():
+            pair_copy(a).start()
+
+    def finish_pair(a):
         if pair[2] == 1:
             return
-        pair_copy(TAPS * TAPS - 1).start()
         mine = place_in(pair) * half
-
-        def wait(ab, carry):
-            pair_copy(ab).wait()
-            return carry
-
-        lax.fori_loop(0, TAPS * TAPS, wait, 0)
+        pair_copy(a).wait()
 
         def add(step, carry):
-            for p in range(parts):
+            for p in range(a * split, (a + 1) * split):
                 total[p, mine + step] = total[p, mine + step] + land_pair[p, step]
             return carry
 
@@ -321,10 +320,10 @@
             sems["gath"] += 1
         return copies
 
-    finish_pair()
     base = place_in(pair) * half
     state = [(base, half)] * parts
     trail = [[] for _ in range(parts)]
+    started = [None] * parts
     depth = len(orders[0])
 
     def small_start(number, group, at):
@@ -350,58 +349,71 @@
             value = value + small_land[pl.ds(slot * SUB, SUB)]
         small_mine[pl.ds((number + 1) * SUB, SUB)] = value
 
-    small_groups = (pair,) + orders[0] + rest
+    def scatter(p, level):
+        if level < depth:
+            trail[p].append(state[p])
+            started[p] = scatter_start(p, orders[p][level], *state[p])
+        else:
+            started[p] = scatter_start(p, rest[level - depth], *state[p], True)
+
+    def end_scatter(p):
+        copies, base, share = started[p]
+        scatter_end(p, copies, base, share)
+        state[p] = (base, share)
+
+    small_groups = (pair, *orders[0], *rest)
     small_at = 0
-    steps = [[order[level] for order in orders] for level in range(depth)]
-    steps += [[group] * parts for group in rest]
-    for level, groups in enumerate(steps):
-        whole = level >= depth
-        started = []
-        for p, group in enumerate(groups):
-            if not whole:
-                trail[p].append(state[p])
-            started.append(scatter_start(p, group, *state[p], whole))
+    for a in range(TAPS):
+        correlate(a)
+        if a == 0:
+            small = small_start(0, small_groups[0], small_at)
+            small_at += len(small)
+        else:
+            finish_pair(a - 1)
+            for p in range((a - 1) * split, a * split):
+                scatter(p, 0)
+    small_end(0, small)
+    finish_pair(TAPS - 1)
+    for p in range(parts - split, parts):
+        scatter(p, 0)
+    levels = depth + len(rest)
+    for level in range(1, levels + 1):
         small = small_start(level, small_groups[level], small_at)
         small_at += len(small)
         for p in range(parts):
-            copies, base, share = started[p]
-            scatter_end(p, copies, base, share)
-            state[p] = (base, share)
+            end_scatter(p)
+            if level < levels:
+                scatter(p, level)
+                continue
+            base, size = state[p]
+
+            def keep(k, carry):
+                value, top = encode(total[p, base + k])
+                full[p, base + k, pl.ds(0, taps)] = value
+                full[p, base + k, taps] = top
+                return carry
+
+            lax.fori_loop(0, size, keep, 0)
+            started[p] = gather_start(p, orders[p][depth - 1], *state[p])
         small_end(level, small)
-    for p in range(parts):
-        base, size = state[p]
-
-        def keep(k, carry):
-            value, top = encode(total[p, base + k])
-            full[p, base + k, pl.ds(0, taps)] = value
-            full[p, base + k, taps] = top
-            return carry
-
-        lax.fori_loop(0, size, keep, 0)
-    last_small = len(steps)
-    small = small_start(last_small, small_groups[last_small], small_at)
+    for k in range(2):
+        small_refs[k][...] = small_mine[pl.ds((levels + 1) * SUB + k, 1)]
     for level in reversed(range(depth)):
-        started = [gather_start(p, orders[p][level], *state[p]) for p in range(parts)]
         for p in range(parts):
             for copy in started[p]:
                 copy.wait()
             state[p] = trail[p][level]
-    small_end(last_small, small)
-    small_ref[...] = small_mine[pl.ds((last_small + 1) * SUB, SUB)]
-    last = []
+            group = orders[p][level - 1] if level else pair
+            started[p] = gather_start(p, group, *state[p])
+    outs = []
     for p in range(parts):
-        last.extend(gather_start(p, pair, *state[p]))
-    here = pl.ds(place_in(pair) * half, half)
-    own = pltpu.make_async_copy(full.at[:, here], out_ref.at[:, here], local_sem.at[2])
-    own.start()
-    for copy in last:
+        for copy in started[p]:
+            copy.wait()
+        copy = pltpu.make_async_copy(full.at[p], out_ref.at[p], out_sem.at[p])
+        copy.start()
+        outs.append(copy)
+    for copy in outs:
         copy.wait()
-    if pair[2] > 1:
-        there = pl.ds((1 - place_in(pair)) * half, half)
-        other = pltpu.make_async_copy(full.at[:, there], out_ref.at[:, there], local_sem.at[3])
-        other.start()
-        other.wait()
-    own.wait()
 
 
 def decode(block, taps):
@@ -409,18 +421,24 @@
     return jnp.log(block[:taps].astype(jnp.float32)) * unit[None]
 
 
-def decode_kernel(code_ref, out_ref):
+def decode_kernel(code_ref, bias_ref, head_ref, out_ref, bias_out, head_out):
     parts, shares, blocks, _, lanes = code_ref.shape
+    taps = blocks - 1
+    split = parts // TAPS
     for p in range(parts):
+        at, lane = p // split * taps, p % split * lanes
         for k in range(shares):
-            out_ref[:, k, :, p * lanes : (p + 1) * lanes] = decode(code_ref[p, k], blocks - 1)
+            out_ref[at : at + taps, k, :, lane : lane + lanes] = decode(code_ref[p, k], taps)
+    bias_out[...] = bias_ref[...]
+    head_out[...] = head_ref[...]
 
 
 def per_device(sizes, clips, weight, bias, head):
     _, frames, _, cols, chans = clips.shape
     count = frames * cols
-    taps, shares, parts = TAPS**3, chans // SUB, 2
-    lanes = chans // parts
+    split = 2
+    taps, shares, parts = TAPS**2, chans // SUB, TAPS * split
+    lanes = chans // split
     plan = make_plan(sizes, shares)
     pair, orders, rest = plan
     half = shares // pair[2]
@@ -442,16 +460,17 @@
     dma = pltpu.SemaphoreType.DMA
     vmem = pl.BlockSpec(memory_space=pltpu.VMEM)
     hbm = pl.BlockSpec(memory_space=pl.ANY)
-    code, small = pl.pallas_call(
+    row = jax.ShapeDtypeStruct((1, chans), jnp.float32)
+    code, *small = pl.pallas_call(
         functools.partial(kernel, sizes, plan),
         out_shape=(
             jax.ShapeDtypeStruct((parts, shares, taps + 1, SUB, lanes), jnp.bfloat16),
-            jax.ShapeDtypeStruct((SUB, chans), jnp.float32),
+            row, row,
         ),
         in_specs=[hbm, hbm, vmem, vmem],
-        out_specs=(hbm, vmem),
+        out_specs=(hbm, vmem, vmem),
         scratch_shapes=[
-            pltpu.VMEM((taps, chans, chans), jnp.bfloat16),
+            pltpu.VMEM((TAPS**3, chans, chans), jnp.bfloat16),
             pad, pad, pad,
             pltpu.VMEM((TAPS, count, chans), jnp.float32),
             field, field,
@@ -463,29 +482,36 @@
             pltpu.VMEM((parts, shares, taps + 1, SUB, lanes), jnp.bfloat16),
             pltpu.VMEM(((len(rest) + 6) * SUB, chans), jnp.float32),
             pltpu.VMEM((max(small_n, 1) * SUB, chans), jnp.float32),
-            dma((4,)), dma((24,)), dma((24,)), dma((TAPS**2,)), dma((TAPS**2,)),
+            dma((2,)), dma((24,)), dma((24,)), dma((TAPS,)), dma((TAPS,)),
             dma((max(parts_n, 1),)), dma((max(parts_n, 1),)),
             dma((max(gath_n, 1),)), dma((max(gath_n, 1),)),
-            dma((max(small_n, 1),)), dma((max(small_n, 1),)),
+            dma((max(small_n, 1),)), dma((max(small_n, 1),)), dma((parts,)),
         ],
         compiler_params=pltpu.CompilerParams(
             collective_id=0, has_side_effects=True, vmem_limit_bytes=60 * 1024 * 1024
         ),
     )(
         clips.reshape(frames, cols, chans),
-        weight.reshape(taps, chans, chans),
+        weight.reshape(TAPS**3, chans, chans),
         bias.reshape(1, chans),
         head.reshape(1, chans),
     )
     step = math.gcd(shares, 4)
-    grad_weight = pl.pallas_call(
+    short = pl.BlockSpec((1, chans), lambda i: (0, 0))
+    grad_weight, grad_bias, grad_head = pl.pallas_call(
         decode_kernel,
-        out_shape=jax.ShapeDtypeStruct((taps, shares, SUB, chans), jnp.float32),
+        out_shape=(jax.ShapeDtypeStruct((TAPS**3, shares, SUB, chans), jnp.float32), row, row),
         grid=(shares // step,),
-        in_specs=[pl.BlockSpec((parts, step, taps + 1, SUB, lanes), lambda i: (0, i, 0, 0, 0))],
-        out_specs=pl.BlockSpec((taps, step, SUB, chans), lambda i: (0, i, 0, 0)),
-    )(code)
-    return grad_weight.reshape(TAPS, TAPS, TAPS, chans, chans), small[0], small[1]
+        in_specs=[
+            pl.BlockSpec((parts, step, taps + 1, SUB, lanes), lambda i: (0, i, 0, 0, 0)),
+            short, short,
+        ],
+        out_specs=(
+            pl.BlockSpec((TAPS**3, step, SUB, chans), lambda i: (0, i, 0, 0)), short, short
+        ),
+    )(code, *small)
+    grad_weight = grad_weight.reshape(TAPS, TAPS, TAPS, chans, chans)
+    return grad_weight, grad_bias.reshape(chans), grad_head.reshape(chans)
 
 
 def solution(mesh):

time: 108 us -> 92.1 us (0.85)
  Pallas kernels: 105 us -> 91.1 us
  local copies, waits for them, and re-layouts: 1.34 us -> 0 us
    pallas_call x1, Pallas kernels: 98 us -> 83.9 us  [per_device(): pl.pallas_call(functools.partial(kernel, sizes, plan), out_shape=(jax.Sha...]
    slice x1 -> x0, local copies, waits for them, and re-layouts: 1.34 us -> none  [per_device(): small[1]]
where the time goes in v3:
time: 92.1 us; the launch traced here: 91.8 us
  Pallas kernels  91.1 us (99%)
    pallas_call x1, Pallas kernels, per_device(): pl.pallas_call(functools.partial(kernel, sizes, plan), out_shape=(jax.Sha...  83.9 us
    pallas_call x1, Pallas kernels, per_device(): pl.pallas_call(decode_kernel, out_shape=(jax.ShapeDtypeStruct((TAPS ** 3,...  7.29 us

profile of v3, /device:TPU:0, one launch (start us, length us, event | category | flops | bytes accessed | tf_op | source)
XLA Modules:
  0.0 91.8 jit_solution(2114151243339487220)
XLA Ops:
  0.6 83.9 %shard_map.67 = (bf16[6,32,10,8,128]{4,3,2,1,0:T(8,128)(2,1)}, f32[1,256]{1,0:T(1,128)}, f32[1,256]{1,0:T(1,128)}) custom-call(bf16[2,128,256]{2,1,0:T(8,128)(2,1)} %bitcast.8, bf16[27,256,256]{2,1,0:T(8,128)(2,1)} %bitcast.7, f32[1,256]{1,0:T(1,128)} %bitcast.9, f32[1,256]{1,0:T(1,128)} %bitcast.10), custom_call_target="tpu_custom_call" | custom-call | tf_op jit(solution)/shard_map/pallas_call | solution.py:464
  84.5 7.3 %shard_map.68 = (f32[27,32,8,256]{3,2,1,0:T(8,128)}, f32[1,256]{1,0:T(1,128)}, f32[1,256]{1,0:T(1,128)}) custom-call(bf16[6,32,10,8,128]{4,3,2,1,0:T(8,128)(2,1)} %get-tuple-element.9.code_ref, f32[1,256]{1,0:T(1,128)} %get-tuple-element.10.bias_ref, f32[1,256]{1,0:T(1,128)} %get-tuple-element.11.head_ref), custom_call_target="tpu_custom_call" | custom-call | tf_op jit(solution)/shard_map/pallas_call | solution.py:501

commit v4 on v3

--- a/solution.py
+++ b/solution.py
@@ -29,7 +29,8 @@
     pair, far, depth, line = cuts
     rest = tuple(group for group in rest if group[2] > 1)
     across, along, ahead = (far, depth, line), (depth, far, line), (line, depth, far)
-    return pair, (ahead, along, across, along, across, across), rest
+    between = (depth, line, far)
+    return pair, (ahead, along, across, between, across, along), rest
 
 
 def kernel(
@@ -496,7 +497,7 @@
         bias.reshape(1, chans),
         head.reshape(1, chans),
     )
-    step = math.gcd(shares, 4)
+    step = math.gcd(shares, 8)
     short = pl.BlockSpec((1, chans), lambda i: (0, 0))
     grad_weight, grad_bias, grad_head = pl.pallas_call(
         decode_kernel,

time: 92.1 us -> 86.5 us (0.939)
  Pallas kernels: 91.1 us -> 85.6 us
    pallas_call x1, Pallas kernels: 83.9 us -> 79.8 us  [per_device(): pl.pallas_call(functools.partial(kernel, sizes, plan), out_shape=(jax.Sha...]
    pallas_call x1, Pallas kernels: 7.29 us -> 5.79 us  [per_device(): pl.pallas_call(decode_kernel, out_shape=(jax.ShapeDtypeStruct((TAPS ** 3,...]
where the time goes in v4:
time: 86.5 us; the launch traced here: 86.2 us
  Pallas kernels  85.6 us (99%)
    pallas_call x1, Pallas kernels, per_device(): pl.pallas_call(functools.partial(kernel, sizes, plan), out_shape=(jax.Sha...  79.8 us
    pallas_call x1, Pallas kernels, per_device(): pl.pallas_call(decode_kernel, out_shape=(jax.ShapeDtypeStruct((TAPS ** 3,...  5.79 us

profile of v4, /device:TPU:0, one launch (start us, length us, event | category | flops | bytes accessed | tf_op | source)
XLA Modules:
  0.0 86.2 jit_solution(17868260394472391210)
XLA Ops:
  0.6 79.8 %shard_map.67 = (bf16[6,32,10,8,128]{4,3,2,1,0:T(8,128)(2,1)}, f32[1,256]{1,0:T(1,128)}, f32[1,256]{1,0:T(1,128)}) custom-call(bf16[2,128,256]{2,1,0:T(8,128)(2,1)} %bitcast.8, bf16[27,256,256]{2,1,0:T(8,128)(2,1)} %bitcast.7, f32[1,256]{1,0:T(1,128)} %bitcast.9, f32[1,256]{1,0:T(1,128)} %bitcast.10), custom_call_target="tpu_custom_call" | custom-call | tf_op jit(solution)/shard_map/pallas_call | solution.py:465
  80.4 5.8 %shard_map.68 = (f32[27,32,8,256]{3,2,1,0:T(8,128)}, f32[1,256]{1,0:T(1,128)}, f32[1,256]{1,0:T(1,128)}) custom-call(bf16[6,32,10,8,128]{4,3,2,1,0:T(8,128)(2,1)} %get-tuple-element.9.code_ref, f32[1,256]{1,0:T(1,128)} %get-tuple-element.10.bias_ref, f32[1,256]{1,0:T(1,128)} %get-tuple-element.11.head_ref), custom_call_target="tpu_custom_call" | custom-call | tf_op jit(solution)/shard_map/pallas_call | solution.py:502

commit v5 on v4

--- a/solution.py
+++ b/solution.py
@@ -30,7 +30,7 @@
     rest = tuple(group for group in rest if group[2] > 1)
     across, along, ahead = (far, depth, line), (depth, far, line), (line, depth, far)
     between = (depth, line, far)
-    return pair, (ahead, along, across, between, across, along), rest
+    return pair, (ahead, across, along, between, across, along), rest
 
 
 def kernel(

time: 86.5 us -> 89.2 us (1.031)
  the two profiles are of different devices: /device:TPU:0 before, /device:TPU:31 now
where the time goes in v5:
time: 89.2 us; the launch traced here: 88.9 us
  Pallas kernels  88.3 us (99%)
    pallas_call x1, Pallas kernels, per_device(): pl.pallas_call(functools.partial(kernel, sizes, plan), out_shape=(jax.Sha...  82.5 us
    pallas_call x1, Pallas kernels, per_device(): pl.pallas_call(decode_kernel, out_shape=(jax.ShapeDtypeStruct((TAPS ** 3,...  5.79 us

profile of v5, /device:TPU:31, one launch (start us, length us, event | category | flops | bytes accessed | tf_op | source)
XLA Modules:
  0.0 88.9 jit_solution(6500130172030430170)
XLA Ops:
  0.6 82.5 %shard_map.67 = (bf16[6,32,10,8,128]{4,3,2,1,0:T(8,128)(2,1)}, f32[1,256]{1,0:T(1,128)}, f32[1,256]{1,0:T(1,128)}) custom-call(bf16[2,128,256]{2,1,0:T(8,128)(2,1)} %bitcast.8, bf16[27,256,256]{2,1,0:T(8,128)(2,1)} %bitcast.7, f32[1,256]{1,0:T(1,128)} %bitcast.9, f32[1,256]{1,0:T(1,128)} %bitcast.10), custom_call_target="tpu_custom_call" | custom-call | tf_op jit(solution)/shard_map/pallas_call | solution.py:465
  83.2 5.8 %shard_map.68 = (f32[27,32,8,256]{3,2,1,0:T(8,128)}, f32[1,256]{1,0:T(1,128)}, f32[1,256]{1,0:T(1,128)}) custom-call(bf16[6,32,10,8,128]{4,3,2,1,0:T(8,128)(2,1)} %get-tuple-element.9.code_ref, f32[1,256]{1,0:T(1,128)} %get-tuple-element.10.bias_ref, f32[1,256]{1,0:T(1,128)} %get-tuple-element.11.head_ref), custom_call_target="tpu_custom_call" | custom-call | tf_op jit(solution)/shard_map/pallas_call | solution.py:502
